TPU v7x, 32 devices: a whole 2x2x4 slice. The times are simulated.
32 devices in a mesh: replica: 2 (over core), model: 4 (over y, x), shift: 4 (over z).
Axes of the slice: x: 2, y: 2, z: 4, core: 2. Of those that a mesh axis runs over, the one named last changes fastest.
Arguments:
- partial_gate: float32 [8, 1024, 3072], P(('shift', 'replica'), None, 'model'), parts along dimension 0, may hold values from -0.875 to 0.875
- partial_up: float32 [8, 1024, 3072], P(('shift', 'replica'), None, 'model'), parts along dimension 0, may hold values from -0.875 to 0.875
- partial_down: float32 [8, 3072, 1024], P(('shift', 'replica'), 'model'), parts along dimension 0, may hold values from -0.875 to 0.875
- partial_norm: float32 [8, 1024], P(('shift', 'replica')), parts along dimension 0, may hold values from -8 to 8
- master_gate: float32 [4096, 3072], P(('shift', 'replica'), 'model'), parts along dimension 0, may hold values from -0.25 to 0.25
- master_up: float32 [4096, 3072], P(('shift', 'replica'), 'model'), parts along dimension 0, may hold values from -0.25 to 0.25
- master_down: float32 [12288, 1024], P(('shift', 'model'), 'replica'), parts along dimension 0, may hold values from -0.15625 to 0.15625
- master_norm: float32 [4096], P(('shift', 'replica')), parts along dimension 0, may hold values from 0.25 to 1.75
- memory_gate: float32 [4096, 3072], P(('shift', 'replica'), 'model'), parts along dimension 0, may hold values from -0.1875 to 0.1875
- memory_up: float32 [4096, 3072], P(('shift', 'replica'), 'model'), parts along dimension 0, may hold values from -0.1875 to 0.1875
- memory_down: float32 [12288, 1024], P(('shift', 'model'), 'replica'), parts along dimension 0, may hold values from -0.109375 to 0.109375
- memory_norm: float32 [4096], P(('shift', 'replica')), parts along dimension 0, may hold values from -1.75 to 1.75
Outputs:
- compute_gate: bfloat16 [4096, 3072], P('shift', 'model'), parts along dimension 0
- compute_up: bfloat16 [4096, 3072], P('shift', 'model'), parts along dimension 0
- compute_down: bfloat16 [12288, 1024], P(('shift', 'model')), parts along dimension 0
- compute_norm: bfloat16 [4096], P('shift'), parts along dimension 0
- stepped_gate: float32 [4096, 3072], P(('shift', 'replica'), 'model'), parts along dimension 0
- stepped_up: float32 [4096, 3072], P(('shift', 'replica'), 'model'), parts along dimension 0
- stepped_down: float32 [12288, 1024], P(('shift', 'model'), 'replica'), parts along dimension 0
- stepped_norm: float32 [4096], P(('shift', 'replica')), parts along dimension 0
- state_new_gate: float32 [4096, 3072], P(('shift', 'replica'), 'model'), parts along dimension 0
- state_new_up: float32 [4096, 3072], P(('shift', 'replica'), 'model'), parts along dimension 0
- state_new_down: float32 [12288, 1024], P(('shift', 'model'), 'replica'), parts along dimension 0
- state_new_norm: float32 [4096], P(('shift', 'replica')), parts along dimension 0
There are 4 independent parts, one for each index of `shift`. A program takes and returns all parts, laid end to end along the dimension named above; each array names one. Nothing has to cross between parts.
All inputs are finite; a program needn't handle non-finite values.
Results may differ from a plain program's by a relative error of at most 0.001.
Values may be sent and summed in bfloat16 or wider, within the bound.
A program may use at most 128 MiB of HBM per device.

v0:
```python
import jax
import jax.numpy as jnp
from jax import lax
from jax.sharding import PartitionSpec as P

learn_rate = 0.5
hold_rate = 0.9


def on_device(
    partial_gate,
    partial_up,
    partial_down,
    partial_norm,
    master_gate,
    master_up,
    master_down,
    master_norm,
    memory_gate,
    memory_up,
    memory_down,
    memory_norm,
):
    mean_gate, mean_up, mean_down = (
        lax.psum_scatter(partial_gate[0], "replica", scatter_dimension=0, tiled=True),
        lax.psum_scatter(partial_up[0], "replica", scatter_dimension=0, tiled=True),
        lax.psum_scatter(partial_down[0], "replica", scatter_dimension=1, tiled=True),
    )
    whole_norm = lax.psum(partial_norm[0], "replica")
    place = lax.axis_index("replica")
    mean_norm = lax.dynamic_slice_in_dim(
        whole_norm, place * master_norm.shape[0], master_norm.shape[0]
    )
    mean_rate = lax.axis_size("replica") ** (-0.5)
    mean_gate = mean_gate * mean_rate
    mean_up = mean_up * mean_rate
    mean_down = mean_down * mean_rate
    mean_norm = mean_norm * mean_rate
    own_gate, own_up, own_down, slope_gate_norm, slope_up_norm, slope_down_norm = lax.psum(
        (
            jnp.sum(master_gate * master_gate, axis=1, keepdims=True),
            jnp.sum(master_up * master_up, axis=1, keepdims=True),
            jnp.sum(master_down * master_down, axis=0, keepdims=True),
            jnp.sum(mean_gate * mean_gate, axis=1, keepdims=True),
            jnp.sum(mean_up * mean_up, axis=1, keepdims=True),
            jnp.sum(mean_down * mean_down, axis=0, keepdims=True),
        ),
        "model",
    )
    mean_gate = mean_gate * (jnp.sqrt(own_gate) * lax.rsqrt(slope_gate_norm + 1e-06))
    mean_up = mean_up * (jnp.sqrt(own_up) * lax.rsqrt(slope_up_norm + 1e-06))
    mean_down = mean_down * (jnp.sqrt(own_down) * lax.rsqrt(slope_down_norm + 1e-06))
    state_new_gate = hold_rate * memory_gate + mean_gate
    stepped_gate = master_gate - learn_rate * state_new_gate
    state_new_up = hold_rate * memory_up + mean_up
    stepped_up = master_up - learn_rate * state_new_up
    state_new_down = hold_rate * memory_down + mean_down
    stepped_down = master_down - learn_rate * state_new_down
    state_new_norm = hold_rate * memory_norm + mean_norm
    stepped_norm = master_norm - learn_rate * state_new_norm
    compute_gate, compute_up, compute_down, compute_norm = (
        lax.all_gather(stepped_gate.astype(jnp.bfloat16), "replica", axis=0, tiled=True),
        lax.all_gather(stepped_up.astype(jnp.bfloat16), "replica", axis=0, tiled=True),
        lax.all_gather(stepped_down.astype(jnp.bfloat16), "replica", axis=1, tiled=True),
        lax.all_gather(stepped_norm.astype(jnp.bfloat16), "replica", axis=0, tiled=True),
    )
    return (
        compute_gate,
        compute_up,
        compute_down,
        compute_norm,
        stepped_gate,
        stepped_up,
        stepped_down,
        stepped_norm,
        state_new_gate,
        state_new_up,
        state_new_down,
        state_new_norm,
    )


def solution(mesh):
    return jax.shard_map(
        on_device,
        mesh=mesh,
        in_specs=(
            P(("shift", "replica"), None, "model"),
            P(("shift", "replica"), None, "model"),
            P(("shift", "replica"), "model", None),
            P(("shift", "replica"), None),
            P(("shift", "replica"), "model"),
            P(("shift", "replica"), "model"),
            P(("shift", "model"), "replica"),
            P(("shift", "replica")),
            P(("shift", "replica"), "model"),
            P(("shift", "replica"), "model"),
            P(("shift", "model"), "replica"),
            P(("shift", "replica")),
        ),
        out_specs=(
            P("shift", "model"),
            P("shift", "model"),
            P(("shift", "model"), None),
            P("shift"),
            P(("shift", "replica"), "model"),
            P(("shift", "replica"), "model"),
            P(("shift", "model"), "replica"),
            P(("shift", "replica")),
            P(("shift", "replica"), "model"),
            P(("shift", "replica"), "model"),
            P(("shift", "model"), "replica"),
            P(("shift", "replica")),
        ),
        check_vma=False,
    )
```

profile of v0, /device:TPU:0, one launch (start us, length us, event | category | flops | bytes accessed | tf_op | source)
XLA Modules:
  0.0 123.3 jit_solution(669578345839216515)
XLA Ops:
  7.2 0.7 reduce-scatter.8.cloned.1.call-update
  8.0 0.7 reduce-scatter.4.cloned.1.call-update
  8.7 0.7 reduce-scatter.6.cloned.1.call-update
  9.4 0.0 all-gather.7.cloned.1.call-start
  9.5 0.7 copy-done.1
  10.1 0.2 multiply_reduce_fusion.5
  10.3 0.6 copy-done
  10.9 0.2 multiply_reduce_fusion.3
  11.1 0.5 copy-done.2
  11.6 0.2 multiply_reduce_fusion.1
  11.8 12.1 %reduce-scatter.8.cloned.1.call-done = f32[768,512]{1,0:T(8,128)} async-done(((f32[768,1024]{1,0:T(8,128)}), f32[768,512]{1,0:T(8,128)}) %reduce-scatter.8.cloned.1.call-update) | async-done | bytes 1572880 | tf_op jit(solution)/shard_map/reduce_scatter | solution.py:27
  23.9 1.6 %multiply_reduce_fusion = f32[512]{0:T(512)S(1)} fusion(f32[768,512]{1,0:T(8,128)} %reduce-scatter.8.cloned.1.call-done), kind=kLoop, calls=%fused_computation.2 | loop fusion | flops 1179136 | bytes 1574912 | tf_op jit(solution)/shard_map/reduce_sum | solution.py:46
  25.6 13.1 %reduce-scatter.4.cloned.1.call-done = f32[512,768]{1,0:T(8,128)} async-done(((f32[1024,768]{1,0:T(8,128)}), f32[512,768]{1,0:T(8,128)}) %reduce-scatter.4.cloned.1.call-update) | async-done | bytes 1572880 | tf_op jit(solution)/shard_map/reduce_scatter | solution.py:25
  38.7 1.6 %multiply_reduce_fusion.4 = f32[512]{0:T(512)S(1)} fusion(f32[512,768]{1,0:T(8,128)} %reduce-scatter.4.cloned.1.call-done), kind=kLoop, calls=%fused_computation.10 | loop fusion | flops 1179136 | bytes 1574912 | tf_op jit(solution)/shard_map/reduce_sum | solution.py:44
  40.3 13.1 %reduce-scatter.6.cloned.1.call-done = f32[512,768]{1,0:T(8,128)} async-done(((f32[1024,768]{1,0:T(8,128)}), f32[512,768]{1,0:T(8,128)}) %reduce-scatter.6.cloned.1.call-update) | async-done | bytes 1572880 | tf_op jit(solution)/shard_map/reduce_scatter | solution.py:26
  53.4 1.6 %multiply_reduce_fusion.2 = f32[512]{0:T(512)S(1)} fusion(f32[512,768]{1,0:T(8,128)} %reduce-scatter.6.cloned.1.call-done), kind=kLoop, calls=%fused_computation.6 | loop fusion | flops 1179136 | bytes 1574912 | tf_op jit(solution)/shard_map/reduce_sum | solution.py:45
  55.0 16.3 %all-reduce = (f32[512,1]{0,1:T(1,128)S(1)}, f32[512,1]{0,1:T(1,128)S(1)}, f32[512,1]{0,1:T(1,128)S(1)}, f32[512,1]{0,1:T(1,128)S(1)}, f32[1,512]{1,0:T(1,128)S(1)}, /*index=5*/f32[1,512]{1,0:T(1,128)S(1)}) all-reduce(f32[512,1]{0,1:T(1,128)S(1)} %bitcast.24, ...), channel_id=1, replica_groups=mesh['replica'=2,'model'=4,'shift'=4] {'model'}, use_global_device_ids=true, to_apply=%region_4.0 | all-reduce | flops 3072 | bytes 24576 | tf_op jit(solution)/shard_map/psum | solution.py:39
  71.4 4.2 %fusion.2 = (bf16[512,768]{1,0:T(8,128)(2,1)}, f32[512,768]{1,0:T(8,128)}, f32[512,768]{1,0:T(8,128)}) fusion(f32[512,768]{1,0:T(8,128)S(1)} %copy-done, f32[512,768]{1,0:T(8,128)} %reduce-scatter.6.cloned.1.call-done, f32[512]{0:T(512)S(1)} %bitcast.26, f32[512,768]{1,0:T(8,128)} %param.21), kind=kLoop, calls=%fused_computation.19 | loop fusion | flops 2359296 | bytes 8652800 | tf_op jit(solution)/shard_map/convert_element_type | solution.py:63
  75.5 0.0 all-gather.5.cloned.1.call-start
  75.6 4.3 %fusion.3 = (bf16[512,768]{1,0:T(8,128)(2,1)}, f32[512,768]{1,0:T(8,128)}, f32[512,768]{1,0:T(8,128)}) fusion(f32[512,768]{1,0:T(8,128)S(1)} %copy-done.1, f32[512,768]{1,0:T(8,128)} %reduce-scatter.4.cloned.1.call-done, f32[512]{0:T(512)S(1)} %bitcast.19, f32[512,768]{1,0:T(8,128)} %param.20), kind=kLoop, calls=%fused_computation.20 | loop fusion | flops 2359296 | bytes 8652800 | tf_op jit(solution)/shard_map/convert_element_type | solution.py:62
  79.9 0.0 all-gather.9.cloned.1.call-start
  80.0 4.8 %fusion.1 = (bf16[768,512]{1,0:T(8,128)(2,1)}, f32[768,512]{1,0:T(8,128)}, f32[768,512]{1,0:T(8,128)}) fusion(f32[768,512]{1,0:T(8,128)S(1)} %copy-done.3, f32[768,512]{1,0:T(8,128)} %reduce-scatter.8.cloned.1.call-done, f32[512]{0:T(512)S(1)} %bitcast.18, f32[768,512]{1,0:T(8,128)} %param.22), kind=kLoop, calls=%fused_computation.18 | loop fusion | flops 2359296 | bytes 8652800 | tf_op jit(solution)/shard_map/convert_element_type | solution.py:64
  84.8 2.5 %psum.55 = f32[1024]{0:T(1024)S(1)} all-reduce(f32[1024]{0:T(1024)S(1)} %bitcast.28), channel_id=1, replica_groups=mesh['replica'=2,'model'=4,'shift'=4] {'replica'}, use_global_device_ids=true, to_apply=%region_15.0 | all-reduce | flops 1024 | bytes 8192 | tf_op jit(solution)/shard_map/psum | solution.py:29
  87.3 0.7 fusion
  88.0 1.8 %all-gather = bf16[2,1,512]{2,1,0:T(2,128)(2,1)S(1)} all-gather(bf16[1,1,512]{2,1,0:T(2,128)(2,1)S(1)} %reshape.30), channel_id=1, replica_groups=mesh['replica'=2,'model'=4,'shift'=4] {'replica'}, dimensions={0}, use_global_device_ids=true | all-gather | bytes 3072 | tf_op jit(solution)/shard_map/all_gather | solution.py:65
  89.8 0.6 copy.24
  90.4 7.1 %all-gather.5.cloned.1.call-done = bf16[1024,768]{1,0:T(8,128)(2,1)} async-done(((bf16[512,768]{1,0:T(8,128)(2,1)}), bf16[1024,768]{1,0:T(8,128)(2,1)}) %all-gather.5.cloned.1.call-update) | async-done | bytes 1572880 | tf_op jit(solution)/shard_map/all_gather | solution.py:62
  97.6 13.0 %all-gather.9.cloned.1.call-done = bf16[768,1024]{1,0:T(8,128)(2,1)} async-done(((bf16[768,512]{1,0:T(8,128)(2,1)}), bf16[768,1024]{1,0:T(8,128)(2,1)}) %all-gather.9.cloned.1.call-update) | async-done | bytes 1572880 | tf_op jit(solution)/shard_map/all_gather | solution.py:64
  110.5 2.8 %copy.28 = bf16[1024,768]{1,0:T(8,128)(2,1)} copy(bf16[1024,768]{1,0:T(8,128)(2,1)} %all-gather.5.cloned.1.call-done) | data formatting | bytes 3145728
  113.3 1.1 copy.29
  114.5 0.8 copy-done.5
  115.3 1.1 copy.30
  (25 shorter events, 0.3 us)
Async XLA Ops:
  7.2 16.8 %reduce-scatter.8.cloned.1.call-start = ((), (), s32[]{:S(2)}) async-start(), calls=%async_computation.7 | async-start | bytes 4718592 | tf_op jit(solution)/shard_map/reduce_scatter | solution.py:27
  7.9 30.8 %reduce-scatter.4.cloned.1.call-start = ((), (), s32[]{:S(2)}) async-start(), calls=%async_computation.3 | async-start | bytes 4718592 | tf_op jit(solution)/shard_map/reduce_scatter | solution.py:25
  8.7 44.7 %reduce-scatter.6.cloned.1.call-start = ((), (), s32[]{:S(2)}) async-start(), calls=%async_computation.5 | async-start | bytes 4718592 | tf_op jit(solution)/shard_map/reduce_scatter | solution.py:26
  8.7 1.4 %copy-start.1 = (f32[512,768]{1,0:T(8,128)S(1)}, f32[512,768]{1,0:T(8,128)}, u32[]{:S(2)}) copy-start(f32[512,768]{1,0:T(8,128)} %param.16) | copy-start | bytes 4718596
  9.4 1.5 %copy-start = (f32[512,768]{1,0:T(8,128)S(1)}, f32[512,768]{1,0:T(8,128)}, u32[]{:S(2)}) copy-start(f32[512,768]{1,0:T(8,128)} %param.17) | copy-start | bytes 4718596
  9.4 81.0 %all-gather.7.cloned.1.call-start = ((), (), s32[]{:S(2)}) async-start(), calls=%async_computation.6 | async-start | bytes 2359296 | tf_op jit(solution)/shard_map/all_gather | solution.py:63
  10.1 1.5 %copy-start.2 = (f32[768,512]{1,0:T(8,128)S(1)}, f32[768,512]{1,0:T(8,128)}, u32[]{:S(2)}) copy-start(f32[768,512]{1,0:T(8,128)} %param.18) | copy-start | bytes 4718596
  75.5 22.0 %all-gather.5.cloned.1.call-start = ((), (), s32[]{:S(2)}) async-start(), calls=%async_computation.4 | async-start | bytes 2359296 | tf_op jit(solution)/shard_map/all_gather | solution.py:62
  75.6 4.4 %copy-start.3 = (f32[768,512]{1,0:T(8,128)S(1)}, f32[768,512]{1,0:T(8,128)}, u32[]{:S(2)}) copy-start(f32[768,512]{1,0:T(8,128)} %param.18) | copy-start | bytes 4718596
  79.9 30.6 %all-gather.9.cloned.1.call-start = ((), (), s32[]{:S(2)}) async-start(), calls=%async_computation.8 | async-start | bytes 2359296 | tf_op jit(solution)/shard_map/all_gather | solution.py:64
  80.0 4.8 %copy-start.6 = (f32[1,1024]{1,0:T(1,128)S(1)}, f32[1,1024]{1,0:T(1,128)}, u32[]{:S(2)}) copy-start(f32[1,1024]{1,0:T(1,128)} %param.15) | copy-start | bytes 12292
  80.0 7.3 %copy-start.7 = (f32[512]{0:T(512)S(1)}, f32[512]{0:T(512)}, u32[]{:S(2)}) copy-start(f32[512]{0:T(512)} %param.19) | copy-start | bytes 6148
  80.0 7.3 %copy-start.8 = (f32[512]{0:T(512)S(1)}, f32[512]{0:T(512)}, u32[]{:S(2)}) copy-start(f32[512]{0:T(512)} %param.23) | copy-start | bytes 6148
  110.5 2.8 %copy-start.4 = (bf16[1024,768]{1,0:T(8,128)(2,1)S(1)}, bf16[1024,768]{1,0:T(8,128)(2,1)}, u32[]{:S(2)}) copy-start(bf16[1024,768]{1,0:T(8,128)(2,1)} %all-gather.7.cloned.1.call-done) | copy-start | bytes 4718596
  113.3 2.0 %copy-start.5 = (bf16[768,1024]{1,0:T(8,128)(2,1)S(1)}, bf16[768,1024]{1,0:T(8,128)(2,1)}, u32[]{:S(2)}) copy-start(bf16[768,1024]{1,0:T(8,128)(2,1)} %all-gather.9.cloned.1.call-done) | copy-start | bytes 4718596
Sparse Core Ops, SparseCore 0:
  10.2 13.6 reduce-scatter.7
  26.2 12.4 reduce-scatter.3
  40.9 12.4 reduce-scatter.5
  75.7 8.8 all-gather.6
  86.5 10.9 all-gather.4
  99.5 10.9 all-gather.8
where the time goes:
time: 124 us; the launch traced here: 123 us
  waiting for transfers between devices  60.6 us (49%)
  blocking collectives  20.6 us (17%)
  other arithmetic  19.3 us (16%)
  between operations  14.2 us (11%)
  local copies, waits for them, and re-layouts  8.34 us (7%)
    psum x1, blocking collectives, on_device(): lax.psum((jnp.sum(master_gate * master_gate, axis=1, keepdims=True), jnp....  16.3 us
    reduce_scatter x1, waiting for transfers between devices, on_device(): lax.psum_scatter(partial_gate[0], 'replica', scatter_dimension=0, tiled=T...  13.1 us
    reduce_scatter x1, waiting for transfers between devices, on_device(): lax.psum_scatter(partial_up[0], 'replica', scatter_dimension=0, tiled=True)  13.1 us
    all_gather x1, waiting for transfers between devices, on_device(): lax.all_gather(stepped_down.astype(jnp.bfloat16), 'replica', axis=1, tile...  13 us
    reduce_scatter x1, waiting for transfers between devices, on_device(): lax.psum_scatter(partial_down[0], 'replica', scatter_dimension=1, tiled=T...  12.1 us
    unnamed x23, local copies, waits for them, and re-layouts  8.34 us
    all_gather x1, waiting for transfers between devices, on_device(): lax.all_gather(stepped_gate.astype(jnp.bfloat16), 'replica', axis=0, tile...  7.15 us
    convert_element_type x1, other arithmetic, on_device(): stepped_down.astype(jnp.bfloat16)  4.77 us
  transfers between devices with their start and end apart: 6, of which 5 were waited for; matrix products, arithmetic and copies ran while one was open for 11% of the time, Pallas kernels for 0%

commit v1 on v0

v1 whole, which is shorter than its diff:
```python
import functools
import math

import jax
import jax.numpy as jnp
from jax import lax
from jax.experimental import pallas as pl
from jax.experimental.pallas import tpu as pltpu
from jax.sharding import PartitionSpec as P

learn_rate = 0.5
hold_rate = 0.9
MESH = pl.DeviceIdType.MESH
LANES = 128


def cut(ref, axis, start, size):
    return ref.at[pl.ds(start, size), :] if axis == 0 else ref.at[:, pl.ds(start, size)]


def kernel(n, m, axes, *refs):
    refs = list(refs)
    take = lambda count: [refs.pop(0) for _ in range(count)]
    t = len(axes)
    partial, (partial_norm,) = take(t), take(1)
    master_hbm, (master_norm,) = take(t), take(1)
    memory_hbm, (memory_norm,) = take(t), take(1)
    compute, (compute_norm,) = take(t), take(1)
    stepped, (stepped_norm,) = take(t), take(1)
    state, (state_norm,) = take(t), take(1)
    got, memory = take(t), take(t)
    master, mean = stepped, state
    mean_n, got_n, master_n, memory_n, whole_n, line_n = take(6)
    own_line, own_got, slope_line, slope_got, fold, tile = take(6)
    load_sem, norm_load_sem = take(2)
    part_send, part_recv, comp_send, comp_recv = take(4)
    own_send, own_recv, slope_send, slope_recv = take(4)
    pn_send, pn_recv, wn_send, wn_recv = take(4)

    me = lax.axis_index("replica")
    at = lax.axis_index("model")
    rate = n ** (-0.5)
    peers = [lax.rem(me + k, n) for k in range(1, n)]
    mates = [lax.rem(at + k, m) for k in range(1, m)]

    chunks = []
    for which, axis in enumerate(axes):
        share = mean[which].shape[axis]
        chunks += [(which, c) for c in range(share // LANES)]
    count = len(chunks)

    def load(kind, number):
        which, c = chunks[number]
        axis = axes[which]
        share = mean[which].shape[axis]
        if kind == 0:
            source = cut(master_hbm[which], axis, c * LANES, LANES)
            target = master[which]
        elif kind == 1:
            start = pl.multiple_of(me * share + c * LANES, LANES)
            source = cut(partial[which].at[0], axis, start, LANES)
            target = mean[which]
        else:
            source = cut(memory_hbm[which], axis, c * LANES, LANES)
            target = memory[which]
        return pltpu.make_async_copy(
            source, cut(target, axis, c * LANES, LANES), load_sem.at[kind, number]
        )

    share_n = mean_n.shape[1]
    norm_loads = [
        pltpu.make_async_copy(
            partial_norm.at[:, pl.ds(pl.multiple_of(me * share_n, LANES), share_n)],
            mean_n,
            norm_load_sem.at[0],
        ),
        pltpu.make_async_copy(master_norm, master_n, norm_load_sem.at[1]),
        pltpu.make_async_copy(memory_norm, memory_n, norm_load_sem.at[2]),
    ]
    barrier = pltpu.get_barrier_semaphore()
    for peer in peers:
        pl.semaphore_signal(barrier, inc=1, device_id={"replica": peer}, device_id_type=MESH)
    for mate in mates:
        pl.semaphore_signal(barrier, inc=1, device_id={"model": mate}, device_id_type=MESH)
    for kind in range(3):
        for number in range(count):
            load(kind, number).start()
    for copy in norm_loads:
        copy.start()
    pl.semaphore_wait(barrier, n - 1 + m - 1)

    def part_copy(number, k):
        which, c = chunks[number]
        axis = axes[which]
        share = mean[which].shape[axis]
        start = pl.multiple_of(peers[k] * share + c * LANES, LANES)
        return pltpu.make_async_remote_copy(
            src_ref=cut(partial[which].at[0], axis, start, LANES),
            dst_ref=cut(got[which].at[k], axis, c * LANES, LANES),
            send_sem=part_send.at[number, k],
            recv_sem=part_recv.at[number, k],
            device_id={"replica": peers[k]},
            device_id_type=MESH,
        )

    def pn_copy(k):
        return pltpu.make_async_remote_copy(
            src_ref=partial_norm.at[
                :, pl.ds(pl.multiple_of(peers[k] * share_n, LANES), share_n)
            ],
            dst_ref=got_n.at[k],
            send_sem=pn_send.at[k],
            recv_sem=pn_recv.at[k],
            device_id={"replica": peers[k]},
            device_id_type=MESH,
        )

    for k in range(n - 1):
        pn_copy(k).start()
    for number in range(count):
        for k in range(n - 1):
            part_copy(number, k).start()

    def folded(square):
        return sum(
            square[:, j : j + LANES] for j in range(0, square.shape[1], LANES)
        )

    def line_of(number, block_of, rows, keep):
        which, c = chunks[number]
        if axes[which] == 0:
            height = 32
            for b in range(LANES // height):
                value = block_of(pl.ds(c * LANES + b * height, height), slice(None))
                if keep is not None:
                    keep[pl.ds(c * LANES + b * height, height), :] = value
                fold[pl.ds(b * height, height), :] = folded(value * value)
            return jnp.sum(fold[...].T, axis=0, keepdims=True)
        height = next(h for h in (128, 64, 32, 16, 8) if rows % h == 0)
        total = jnp.zeros((8, LANES), jnp.float32)
        lanes = pl.ds(c * LANES, LANES)
        for b in range(rows // height):
            value = block_of(pl.ds(b * height, height), lanes)
            if keep is not None:
                keep[pl.ds(b * height, height), lanes] = value
            total = total + jnp.sum((value * value).reshape(height // 8, 8, LANES), axis=0)
        return jnp.sum(total, axis=0, keepdims=True)

    def own_copy(k):
        return pltpu.make_async_remote_copy(
            src_ref=own_line,
            dst_ref=own_got.at[k],
            send_sem=own_send.at[k],
            recv_sem=own_recv.at[k],
            device_id={"model": mates[k]},
            device_id_type=MESH,
        )

    for number in range(count):
        which, c = chunks[number]
        load(0, number).wait()
        own_line[number] = line_of(
            number, lambda r, l: master[which][r, l], master[which].shape[0], None
        )
    for k in range(m - 1):
        own_copy(k).start()

    def wn_copy(k):
        mine = whole_n.at[:, pl.ds(pl.multiple_of(me * share_n, LANES), share_n)]
        return pltpu.make_async_remote_copy(
            src_ref=mine,
            dst_ref=mine,
            send_sem=wn_send.at[k],
            recv_sem=wn_recv.at[k],
            device_id={"replica": peers[k]},
            device_id_type=MESH,
        )

    for copy in norm_loads:
        copy.wait()
    total = mean_n[...]
    for k in range(n - 1):
        pn_copy(k).wait()
        total = total + got_n[k]
    new = hold_rate * memory_n[...] + total * rate
    state_norm[...] = new
    new = master_n[...] - learn_rate * new
    stepped_norm[...] = new
    whole_n[:, pl.ds(pl.multiple_of(me * share_n, LANES), share_n)] = new
    for k in range(n - 1):
        wn_copy(k).start()

    def slope_copy(number, k):
        return pltpu.make_async_remote_copy(
            src_ref=slope_line.at[number],
            dst_ref=slope_got.at[number, k],
            send_sem=slope_send.at[number, k],
            recv_sem=slope_recv.at[number, k],
            device_id={"model": mates[k]},
            device_id_type=MESH,
        )

    def reduce(number):
        which, c = chunks[number]
        load(1, number).wait()
        for k in range(n - 1):
            part_copy(number, k).wait_recv()

        def block(r, l):
            value = mean[which][r, l]
            for k in range(n - 1):
                value = value + got[which][k, r, l]
            return value * rate

        slope_line[number] = line_of(number, block, mean[which].shape[0], mean[which])
        for k in range(m - 1):
            slope_copy(number, k).start()

    def comp_copy(number, k):
        which, c = chunks[number]
        axis = axes[which]
        share = mean[which].shape[axis]
        mine = cut(compute[which], axis, pl.multiple_of(me * share + c * LANES, LANES), LANES)
        return pltpu.make_async_remote_copy(
            src_ref=mine,
            dst_ref=mine,
            send_sem=comp_send.at[number, k],
            recv_sem=comp_recv.at[number, k],
            device_id={"replica": peers[k]},
            device_id_type=MESH,
        )

    def update(number):
        which, c = chunks[number]
        axis = axes[which]
        share = mean[which].shape[axis]
        own, slope = own_line[number], slope_line[number]
        for k in range(m - 1):
            slope_copy(number, k).wait_recv()
            own = own + own_got[k, number]
            slope = slope + slope_got[number, k]
        ratio = jnp.sqrt(own) * lax.rsqrt(slope + 1e-06)
        load(2, number).wait()
        base = pl.multiple_of(me * share, LANES)

        def finish(r, l, r_out, l_out, scale):
            new = hold_rate * memory[which][r, l] + mean[which][r, l] * scale
            state[which][r, l] = new
            new = master[which][r, l] - learn_rate * new
            stepped[which][r, l] = new
            compute[which][r_out, l_out] = new.astype(jnp.bfloat16)

        if axis == 0:
            tile[...] = jnp.broadcast_to(ratio, (LANES, LANES)).T
            height, width = 32, mean[which].shape[1]
            for b in range(LANES // height):
                first = c * LANES + b * height
                finish(
                    pl.ds(first, height),
                    slice(None),
                    pl.ds(pl.multiple_of(base + first, height), height),
                    slice(None),
                    jnp.concatenate(
                        [tile[pl.ds(b * height, height), :]] * (width // LANES), axis=1
                    ),
                )
        else:
            rows = mean[which].shape[0]
            height = next(h for h in (128, 64, 32, 16, 8) if rows % h == 0)
            for b in range(rows // height):
                r = pl.ds(b * height, height)
                finish(
                    r,
                    pl.ds(c * LANES, LANES),
                    r,
                    pl.ds(pl.multiple_of(base + c * LANES, LANES), LANES),
                    ratio,
                )
        for k in range(n - 1):
            comp_copy(number, k).start()

    ahead = 4
    for number in range(count + ahead):
        if number < count:
            reduce(number)
        if number == ahead:
            for k in range(m - 1):
                own_copy(k).wait()
        if number >= ahead:
            update(number - ahead)

    for k in range(n - 1):
        wn_copy(k).wait()
    for j in range(whole_n.shape[1] // LANES):
        line_n[pl.ds(j, 1), :] = whole_n[:, j * LANES : (j + 1) * LANES]
    compute_norm[...] = line_n[...].astype(jnp.bfloat16)
    for number in range(count):
        for k in range(n - 1):
            part_copy(number, k).wait_send()
            comp_copy(number, k).wait()
        for k in range(m - 1):
            slope_copy(number, k).wait_send()


def drain(*refs):
    half = len(refs) // 2
    sems = refs[-1]
    copies = [
        pltpu.make_async_copy(refs[i], refs[half + i], sems.at[i]) for i in range(half)
    ]
    for copy in copies:
        copy.start()
    for copy in copies:
        copy.wait()


def exchange(n, m, args):
    axes = (0, 0, 1)
    partial, partial_norm = args[0:3], args[3]
    master, master_norm = args[4:7], args[7]
    memory, memory_norm = args[8:11], args[11]
    row = lambda x: x.reshape(1, -1)
    shapes = [x.shape for x in master]
    count = sum(s[a] // LANES for s, a in zip(shapes, axes))
    share_n, width_n = master_norm.shape[0], partial_norm.shape[1]
    f32, bf16 = jnp.float32, jnp.bfloat16
    dma = lambda *s: pltpu.SemaphoreType.DMA(s)
    out_shape = (
        [pltpu.VMEM(x.shape[1:], bf16) for x in partial]
        + [pltpu.VMEM((width_n // LANES, LANES), bf16)]
        + ([pltpu.VMEM(s, f32) for s in shapes] + [pltpu.VMEM((1, share_n), f32)]) * 2
    )
    scratch = (
        [pltpu.VMEM((n - 1,) + s, f32) for s in shapes]
        + [pltpu.VMEM(s, f32) for s in shapes]
        + [
            pltpu.VMEM((1, share_n), f32),
            pltpu.VMEM((n - 1, 1, share_n), f32),
            pltpu.VMEM((1, share_n), f32),
            pltpu.VMEM((1, share_n), f32),
            pltpu.VMEM((1, width_n), f32),
            pltpu.VMEM((width_n // LANES, LANES), f32),
            pltpu.VMEM((count, 1, LANES), f32),
            pltpu.VMEM((m - 1, count, 1, LANES), f32),
            pltpu.VMEM((count, 1, LANES), f32),
            pltpu.VMEM((count, m - 1, 1, LANES), f32),
            pltpu.VMEM((LANES, LANES), f32),
            pltpu.VMEM((LANES, LANES), f32),
            dma(3, count),
            dma(3),
        ]
        + [dma(count, n - 1)] * 4
        + [dma(m - 1)] * 2
        + [dma(count, m - 1)] * 2
        + [dma(n - 1)] * 4
    )
    results = sum(math.prod(x.shape) * jnp.dtype(x.dtype).itemsize for x in out_shape)
    room = 63 * 2**20 - results
    outs = pl.pallas_call(
        functools.partial(kernel, n, m, axes),
        out_shape=out_shape,
        in_specs=[pl.BlockSpec(memory_space=pltpu.HBM)] * 12,
        out_specs=[pl.BlockSpec(memory_space=pltpu.VMEM)] * 12,
        scratch_shapes=scratch,
        compiler_params=pltpu.CompilerParams(
            collective_id=0, has_side_effects=True, vmem_limit_bytes=room
        ),
    )(
        *partial, partial_norm, *master, row(master_norm), *memory, row(memory_norm)
    )
    outs = pl.pallas_call(
        drain,
        out_shape=[jax.ShapeDtypeStruct(x.shape, x.dtype) for x in outs],
        in_specs=[pl.BlockSpec(memory_space=pl.ANY)] * len(outs),
        out_specs=[pl.BlockSpec(memory_space=pltpu.HBM)] * len(outs),
        scratch_shapes=[dma(len(outs))],
        compiler_params=pltpu.CompilerParams(vmem_limit_bytes=2**20),
    )(*outs)
    return [x.reshape(-1) if i % 4 == 3 else x for i, x in enumerate(outs)]


def plain(args):
    partial, master, memory = args[0:4], args[4:8], args[8:12]
    n = lax.axis_size("replica")
    axes = (0, 0, 1, 0)
    mean = [
        lax.psum_scatter(p[0], "replica", scatter_dimension=a, tiled=True) * n ** (-0.5)
        for p, a in zip(partial, axes)
    ]
    square = lambda x, a: jnp.sum(x * x, axis=1 - a, keepdims=True)
    own, slope = lax.psum(
        (
            [square(x, a) for x, a in zip(master[:3], axes)],
            [square(x, a) for x, a in zip(mean[:3], axes)],
        ),
        "model",
    )
    mean = [
        x * (jnp.sqrt(o) * lax.rsqrt(s + 1e-06)) for x, o, s in zip(mean[:3], own, slope)
    ] + mean[3:]
    state = [hold_rate * e + x for e, x in zip(memory, mean)]
    stepped = [w - learn_rate * s for w, s in zip(master, state)]
    compute = [
        lax.all_gather(s.astype(jnp.bfloat16), "replica", axis=a, tiled=True)
        for s, a in zip(stepped, axes)
    ]
    return compute + stepped + state


def on_device(*args):
    n, m = lax.axis_size("replica"), lax.axis_size("model")
    shares = (args[4].shape[0], args[5].shape[0], args[6].shape[1], args[7].shape[0])
    if n > 1 and m > 1 and all(s % LANES == 0 for s in shares):
        return tuple(exchange(n, m, args))
    return tuple(plain(args))


def solution(mesh):
    partial = P(("shift", "replica"), None, "model")
    rows, columns = P(("shift", "replica"), "model"), P(("shift", "model"), "replica")
    vector = P(("shift", "replica"))
    own = (rows, rows, columns, vector)
    return jax.shard_map(
        on_device,
        mesh=mesh,
        in_specs=(
            partial,
            partial,
            P(("shift", "replica"), "model", None),
            P(("shift", "replica"), None),
        )
        + own
        + own,
        out_specs=(
            P("shift", "model"),
            P("shift", "model"),
            P(("shift", "model"), None),
            P("shift"),
        )
        + own
        + own,
        check_vma=False,
    )
```

time: 124 us -> 26.2 us (0.21)
  waiting for transfers between devices: 60.6 us -> 0 us
  Pallas kernels: 0 us -> 25.4 us
  blocking collectives: 20.6 us -> 0 us
  other arithmetic: 19.3 us -> 0 us
  between operations: 14.2 us -> 0.66 us
  local copies, waits for them, and re-layouts: 8.34 us -> 0 us
    reduce_scatter x3 -> x0, waiting for transfers between devices: 38.3 us -> none  [the longest x1 13.1 us: on_device(): lax.psum_scatter(partial_gate[0], 'replica', scatter_dimension=0, tiled=T...]
    pallas_call x0 -> x2, Pallas kernels: none -> 25.4 us  [the longest x1 20.2 us: exchange(): pl.pallas_call(functools.partial(kernel, n, m, axes), out_shape=out_shape...]
    all_gather x3 -> x0, waiting for transfers between devices: 20.1 us -> none  [the longest x1 13 us: on_device(): lax.all_gather(stepped_down.astype(jnp.bfloat16), 'replica', axis=1, tile...]
    psum x2 -> x0, blocking collectives: 18.8 us -> none  [the longest x1 16.3 us: on_device(): lax.psum((jnp.sum(master_gate * master_gate, axis=1, keepdims=True), jnp....]
    convert_element_type x4 -> x0, other arithmetic: 13.9 us -> none  [the longest x1 4.77 us: on_device(): stepped_down.astype(jnp.bfloat16)]
    unnamed x23 -> x0, local copies, waits for them, and re-layouts: 8.34 us -> none
    reduce_sum x6 -> x0, other arithmetic: 5.41 us -> none  [the longest x1 1.64 us: on_device(): jnp.sum(mean_up * mean_up, axis=1, keepdims=True)]
    unnamed x6 -> x0, waiting for transfers between devices: 2.1 us -> none
  transfers between devices with their start and end apart: 6 -> 0, of which waited for: 5 -> 0; matrix products, arithmetic and copies ran while one was open for 11% -> 0% of each run, Pallas kernels for 0% -> 0%
where the time goes in v1:
time: 26.2 us; the launch traced here: 26.1 us
  Pallas kernels  25.4 us (97%)
  between operations  0.66 us (3%)
    pallas_call x1, Pallas kernels, exchange(): pl.pallas_call(functools.partial(kernel, n, m, axes), out_shape=out_shape...  20.2 us
    pallas_call x1, Pallas kernels, exchange(): pl.pallas_call(drain, out_shape=[jax.ShapeDtypeStruct(x.shape, x.dtype) f...  5.19 us

profile of v1, /device:TPU:0, one launch (start us, length us, event | category | flops | bytes accessed | tf_op | source)
XLA Modules:
  0.0 26.1 jit_solution(6215148576358806053)
XLA Ops:
  0.6 20.2 %shard_map.211 = (bf16[1024,768]{1,0:T(8,128)(2,1)S(1)}, bf16[1024,768]{1,0:T(8,128)(2,1)S(1)}, bf16[768,1024]{1,0:T(8,128)(2,1)S(1)}, bf16[8,128]{1,0:T(8,128)(...) custom-call(f32[1,1024,768]{2,1,0:T(8,128)} %refs_0_.1, ...), custom_call_target="tpu_custom_call" | custom-call | tf_op jit(solution)/shard_map/pallas_call | solution.py:359
  20.9 5.2 %shard_map.212 = (bf16[1024,768]{1,0:T(8,128)(2,1)}, bf16[1024,768]{1,0:T(8,128)(2,1)}, bf16[768,1024]{1,0:T(8,128)(2,1)}, bf16[8,128]{1,0:T(8,128)(2,1)}, f32[5...) custom-call(bf16[1024,768]{1,0:T(8,128)(2,1)S(1)} %get-tuple-element, ...), custom_call_target="tpu_custom_call" | custom-call | tf_op jit(solution)/shard_map/pallas_call | solution.py:371

commit v2 on v1

--- a/solution.py
+++ b/solution.py
@@ -279,7 +279,7 @@
         for k in range(n - 1):
             comp_copy(number, k).start()
 
-    ahead = 4
+    ahead = 8
     for number in range(count + ahead):
         if number < count:
             reduce(number)

time: 26.2 us -> 23.1 us (0.88)
  Pallas kernels: 25.4 us -> 22.3 us
    pallas_call x1, Pallas kernels: 20.2 us -> 17.1 us  [exchange(): pl.pallas_call(functools.partial(kernel, n, m, axes), out_shape=out_shape...]
where the time goes in v2:
time: 23.1 us; the launch traced here: 22.9 us
  Pallas kernels  22.3 us (97%)
  between operations  0.66 us (3%)
    pallas_call x1, Pallas kernels, exchange(): pl.pallas_call(functools.partial(kernel, n, m, axes), out_shape=out_shape...  17.1 us
    pallas_call x1, Pallas kernels, exchange(): pl.pallas_call(drain, out_shape=[jax.ShapeDtypeStruct(x.shape, x.dtype) f...  5.19 us

profile of v2, /device:TPU:0, one launch (start us, length us, event | category | flops | bytes accessed | tf_op | source)
XLA Modules:
  0.0 22.9 jit_solution(2356192947406264631)
XLA Ops:
  0.6 17.1 %shard_map.211 = (bf16[1024,768]{1,0:T(8,128)(2,1)S(1)}, bf16[1024,768]{1,0:T(8,128)(2,1)S(1)}, bf16[768,1024]{1,0:T(8,128)(2,1)S(1)}, bf16[8,128]{1,0:T(8,128)(...) custom-call(f32[1,1024,768]{2,1,0:T(8,128)} %refs_0_.1, ...), custom_call_target="tpu_custom_call" | custom-call | tf_op jit(solution)/shard_map/pallas_call | solution.py:359
  17.7 5.2 %shard_map.212 = (bf16[1024,768]{1,0:T(8,128)(2,1)}, bf16[1024,768]{1,0:T(8,128)(2,1)}, bf16[768,1024]{1,0:T(8,128)(2,1)}, bf16[8,128]{1,0:T(8,128)(2,1)}, f32[5...) custom-call(bf16[1024,768]{1,0:T(8,128)(2,1)S(1)} %get-tuple-element, ...), custom_call_target="tpu_custom_call" | custom-call | tf_op jit(solution)/shard_map/pallas_call | solution.py:371
